TPU v7x, 256 devices: a whole 4x4x8 slice. The times are simulated.
256 devices in a mesh: ep: 64 (over z, x, core), tp: 4 (over y).
Axes of the slice: x: 4, y: 4, z: 8, core: 2. Of those that a mesh axis runs over, the one named last changes fastest.
Arguments:
- tokens: bfloat16 [16384, 2048], P('ep', 'tp'), may hold values from -180 to 180
- norm_gain: float32 [2048], replicated, may hold values from 0.1 to 1.9
- router_weight: bfloat16 [2048, 60], P('tp'), may hold values from -2 to 2
- shared_gate_w: bfloat16 [2048], replicated, may hold values from -0.125 to 0.125
- expert_ids: int32 [16384, 4], P('ep'), may hold values from 0 to 59, all different within a row; in each aligned block of 256 rows (0 to 255, 256 to 511, ...) at most 32 rows name the same one
- w_gate: bfloat16 [64, 2048, 1408], P('ep', None, 'tp'), may hold values from -0.125 to 0.125
- w_up: bfloat16 [64, 2048, 1408], P('ep', None, 'tp'), may hold values from -0.125 to 0.125
- w_down: bfloat16 [64, 1408, 2048], P('ep', 'tp'), may hold values from -1.5 to 1.5
- shared_w_gate: bfloat16 [2048, 2816], P(None, 'tp'), may hold values from -0.125 to 0.125
- shared_w_up: bfloat16 [2048, 2816], P(None, 'tp'), may hold values from -0.125 to 0.125
- shared_w_down: bfloat16 [2816, 2048], P('tp'), may hold values from -0.109375 to 0.109375
Outputs:
- moe_out: bfloat16 [16384, 2048], P('ep', 'tp')
Inputs may be any that keep to these rules, and one draw needn't show every extreme that they name: `expert_ids`: each row names 4 different experts below 60. Within the 256 rows of one index of ep no expert is named by more than 32 rows, and in some of these blocks one expert is named by exactly 32 rows.
All inputs are finite; a program needn't handle non-finite values.
Results may differ from a plain program's by a relative error of at most 0.0069.
Values may be sent and summed in bfloat16 or wider, within the bound.
No kernel may reach another device: no remote copies, remote signals or barrier semaphores. Data moves between devices by JAX's collectives and lax.ppermute only.
A program may use at most 128 MiB of HBM per device.

v0:
```python
import jax
import jax.numpy as jnp
from jax import lax
from jax.sharding import PartitionSpec as P


def laid_out(parts, dim):
    lengths = list(parts.shape[1:])
    lengths[dim] *= parts.shape[0]
    return jnp.moveaxis(parts, 0, dim).reshape(lengths)


def copy_for_each(value, axis):
    peers = lax.axis_size(axis)
    return lax.all_to_all(
        jnp.broadcast_to(value[None], (peers, *value.shape)), axis, 0, 0, tiled=True
    )


def collect(value, axis, dim):
    return laid_out(copy_for_each(value, axis), dim)


def taken_together(value, axis):
    return copy_for_each(value, axis).sum(axis=0)


def turned_gather(arrays, axis, dims):
    turned = [jnp.moveaxis(a, dim, 0) for a, dim in zip(arrays, dims)]
    both = jnp.concatenate([t.reshape(len(t), -1) for t in turned], axis=1)
    out, at, done = (lax.all_gather(both, axis, axis=0, tiled=True), 0, [])
    for t, dim in zip(turned, dims):
        piece = out[:, at : at + t[0].size].reshape(-1, *t.shape[1:])
        done.append(jnp.moveaxis(piece, 0, dim))
        at += t[0].size
    return tuple(done)


def cut_along(value, dim, peers):
    before, after = (value.shape[:dim], value.shape[dim + 1 :])
    return jnp.moveaxis(value.reshape(*before, peers, -1, *after), dim, 0)


def sent_and_summed(value, axis, dim):
    peers = lax.axis_size(axis)
    parts = lax.all_to_all(cut_along(value, dim, peers), axis, 0, 0, tiled=True)
    return jnp.sum(parts.astype(jnp.float32), axis=0)


def send_back(summed):
    return lax.all_to_all(summed, "ep", split_axis=0, concat_axis=0, tiled=True)


def expert_rows(arrived, w_gate, w_up, w_down):
    share = arrived.shape[0] // lax.axis_size("tp")
    mine = lax.dynamic_slice_in_dim(arrived, lax.axis_index("tp") * share, share, 0)
    gate_act = jnp.einsum("sekd,edf->sekf", mine, w_gate, preferred_element_type=jnp.float32)
    up_act = jnp.einsum("sekd,edf->sekf", mine, w_up, preferred_element_type=jnp.float32)
    hidden = (jax.nn.silu(gate_act) * up_act).astype(jnp.bfloat16)
    full_out = jnp.einsum(
        "sekf,efd->sekd", hidden, w_down, preferred_element_type=jnp.float32
    ).astype(jnp.bfloat16)
    summed = lax.all_to_all(full_out, "tp", split_axis=3, concat_axis=0, tiled=True)
    return send_back(summed)


def per_device(
    tokens,
    norm_gain,
    router_weight,
    shared_gate_w,
    expert_ids,
    w_gate,
    w_up,
    w_down,
    shared_w_gate,
    shared_w_up,
    shared_w_down,
):
    width = tokens.shape[1]
    tok_rows = tokens.shape[0]
    column_start = lax.axis_index("tp") * width
    whole = collect(tokens, "tp", 1)
    values = whole.astype(jnp.float32)
    inv_rms = lax.rsqrt(jnp.mean(values * values, axis=-1, keepdims=True) + 1e-06)
    normed = (values * inv_rms * norm_gain[None, :]).astype(jnp.bfloat16)
    own_part = lax.dynamic_slice_in_dim(normed, column_start, width, 1)
    partial_logits = jnp.dot(own_part, router_weight, preferred_element_type=jnp.float32)
    logits = taken_together(partial_logits, "tp")
    probs = jax.nn.softmax(logits, axis=-1)
    expert_count = logits.shape[1]
    matches = expert_ids[:, :, None] == jnp.arange(expert_count, dtype=jnp.int32)[None, None, :]
    route_weight = jnp.sum(jnp.where(matches, probs[:, None, :], 0.0), axis=-1)
    gate_whole, up_whole = turned_gather((w_gate, w_up), "tp", (2, 2))
    down_whole = lax.all_gather(w_down, "tp", axis=1, tiled=True)
    experts_here = w_gate.shape[0]
    slot_count = lax.axis_size("ep") * experts_here
    capacity = tok_rows // 8
    flat_ids = expert_ids.reshape(-1)
    one_hot = (flat_ids[:, None] == jnp.arange(slot_count, dtype=jnp.int32)[None, :]).astype(
        jnp.int32
    )
    before = jnp.cumsum(one_hot, axis=0) - one_hot
    order_rank = jnp.sum(before * one_hot, axis=1)
    slot_ids = (flat_ids * capacity + order_rank).reshape(expert_ids.shape)
    targets = jnp.arange(slot_count * capacity, dtype=jnp.int32)
    dispatch_map = jnp.sum(
        (slot_ids[None, :, :] == targets[:, None, None]).astype(jnp.bfloat16), axis=2
    )
    outgoing = jnp.dot(dispatch_map, normed, preferred_element_type=jnp.float32).astype(
        jnp.bfloat16
    )
    outgoing = outgoing.reshape(lax.axis_size("ep"), experts_here, capacity, normed.shape[1])
    returned = expert_rows(
        lax.all_to_all(outgoing, "ep", split_axis=0, concat_axis=0, tiled=True),
        w_gate=gate_whole,
        w_up=up_whole,
        w_down=down_whole,
    )
    picked = returned.reshape(slot_count * capacity, width)[slot_ids]
    routed = jnp.sum(route_weight[:, :, None] * picked.astype(jnp.float32), axis=1)
    shared_gate_act = jnp.dot(normed, shared_w_gate, preferred_element_type=jnp.float32)
    shared_up_act = jnp.dot(normed, shared_w_up, preferred_element_type=jnp.float32)
    shared_hidden = (jax.nn.silu(shared_gate_act) * shared_up_act).astype(jnp.bfloat16)
    shared_part = jnp.dot(shared_hidden, shared_w_down, preferred_element_type=jnp.float32)
    shared_own = sent_and_summed(shared_part.astype(jnp.bfloat16), "tp", 1)
    share_gate = jax.nn.sigmoid(jnp.dot(normed, shared_gate_w, preferred_element_type=jnp.float32))
    return (share_gate[:, None] * shared_own + routed).astype(jnp.bfloat16)


def solution(mesh):
    return jax.shard_map(
        per_device,
        mesh=mesh,
        in_specs=(
            P("ep", "tp"),
            P(),
            P("tp", None),
            P(),
            P("ep", None),
            P("ep", None, "tp"),
            P("ep", None, "tp"),
            P("ep", "tp", None),
            P(None, "tp"),
            P(None, "tp"),
            P("tp", None),
        ),
        out_specs=P("ep", "tp"),
        check_vma=False,
    )
```

profile of v0, /device:TPU:8, one launch (start us, length us, event | category | flops | bytes accessed | tf_op | source)
XLA Modules:
  0.0 429.5 jit_solution(3899483268526843282)
XLA Ops:
  6.5 0.0 copy-start
  6.5 0.0 all-gather.3.cloned.1.call-start
  6.5 3.8 pad_maximum_fusion
  10.4 0.0 all-gather.3.cloned.1.call-update
  10.4 0.9 copy-done.3
  11.3 0.1 copy.93
  11.4 1.0 broadcast_in_dim.14
  12.5 6.4 %all-to-all-start = ((bf16[4,256,512]{1,2,0:T(8,128)(2,1)}), bf16[4,256,512]{1,2,0:T(8,128)(2,1)}, u32[]{:S(2)}, u32[]{:S(2)}) async-start(bf16[4,256,512]{1,2,0:T(8,128)(2,1)} %broadcast_in_dim.14), calls=%async_computation | async-start | bytes 2097152 | tf_op jit(solution)/shard_map/all_to_all | solution.py:15
  18.8 0.0 copy-done.5
  18.8 0.1 copy.97
  19.0 0.1 eq.58
  19.1 0.1 eq.54
  19.2 18.0 %reduce-window.6 = s32[64,8,128]{2,1,0:T(8,128)S(1)} reduce-window(s32[64,8,128]{2,1,0:T(8,128)S(1)} %fusion.47, s32[]{:T(128)} %constant.8.clone.1), window={size=1x1x128 pad=0_0x0_0x127_0}, to_apply=%region_6.7 | reduce-window | flops 8323072 | bytes 524292 | tf_op jit(solution)/shard_map/reduce-window
  37.3 0.1 slice.19
  37.4 0.1 copy.99
  37.6 0.1 copy.100
  37.7 0.1 broadcast_add_fusion
  37.8 0.1 fusion.44
  37.9 0.1 reduce_sum.83
  38.0 0.1 copy.101
  38.1 2.5 fusion.7
  40.6 0.0 all-to-all-done
  40.7 1.6 multiply_reduce_fusion.1
  42.3 1.6 fusion.32
  43.9 5.8 %convolution_convert_fusion = bf16[2048,2048]{1,0:T(8,128)(2,1)} fusion(bf16[2048,256]{1,0:T(8,128)(2,1)S(1)} %copy-done.2, bf16[256,2048]{0,1:T(8,128)(2,1)S(1)} %fusion.32), kind=kOutput, calls=%fused_computation.3 | convolution fusion | flops 2151677952 | bytes 10485760 | tf_op jit(solution)/shard_map/dot_general | solution.py:110
  49.7 0.0 copy-done.1
  49.7 10.9 %all-to-all-start.3 = ((bf16[64,1,32,2048]{3,2,1,0:T(8,128)(2,1)}), bf16[64,1,32,2048]{3,2,1,0:T(8,128)(2,1)}, u32[]{:S(2)}, u32[]{:S(2)}) async-start(bf16[64,1,32,2048]{3,2,1,0:T(8,128)(2,1)} %bitcast.131), calls=%async_computation.3 | async-start | bytes 16777216 | tf_op jit(solution)/shard_map/all_to_all | solution.py:115
  60.6 0.0 all-gather.5.cloned.1.call-start
  60.6 0.7 all-gather.5.cloned.1.call-update
  61.4 1.1 fusion.45
  62.5 63.2 %all-gather.3.cloned.1.call-done = bf16[1408,4096]{1,0:T(8,128)(2,1)} async-done(((bf16[352,4096]{1,0:T(8,128)(2,1)}), bf16[1408,4096]{1,0:T(8,128)(2,1)}) %all-gather.3.cloned.1.call-update) | async-done | bytes 11534352 | tf_op jit(solution)/shard_map/all_gather | solution.py:31
  125.7 11.0 %fusion.56 = (bf16[1408,2048]{1,0:T(8,128)(2,1)}, bf16[1408,2048]{1,0:T(8,128)(2,1)}) fusion(bf16[1408,4096]{1,0:T(8,128)(2,1)} %all-gather.3.cloned.1.call-done), kind=kLoop, calls=%fused_computation.61 | loop fusion | bytes 23068672 | tf_op jit(solution)/shard_map/slice | solution.py:33
  136.6 8.5 %copy.110 = bf16[1408,2048]{0,1:T(8,128)(2,1)} copy(bf16[1408,2048]{1,0:T(8,128)(2,1)} %get-tuple-element.7) | data formatting | bytes 11534336
  145.2 8.4 %copy.111 = bf16[1408,2048]{0,1:T(8,128)(2,1)} copy(bf16[1408,2048]{1,0:T(8,128)(2,1)} %get-tuple-element.8) | data formatting | bytes 11534336
  153.5 93.2 %all-to-all-done.3 = bf16[64,1,32,2048]{3,2,1,0:T(8,128)(2,1)} async-done(((bf16[64,1,32,2048]{3,2,1,0:T(8,128)(2,1)}), bf16[64,1,32,2048]{3,2,1,0:T(8,128)(2,1)}, u32[]{:S(2)}, u32[]{:S(2)}) %all-to-all-start.3) | async-done | bytes 8388640 | tf_op jit(solution)/shard_map/all_to_all | solution.py:115
  246.8 0.7 broadcast_in_dim.15
  247.5 4.8 %all-to-all-start.2 = ((f32[4,256,60]{1,2,0:T(8,128)}), f32[4,256,60]{1,2,0:T(8,128)S(1)}, u32[]{:S(2)}, u32[]{:S(2)}) async-start(f32[4,256,60]{1,2,0:T(8,128)} %broadcast_in_dim.15), calls=%async_computation.2 | async-start | bytes 524288 | tf_op jit(solution)/shard_map/all_to_all | solution.py:15
  252.3 8.3 %fusion.8 = f32[16,1,32,1408]{3,2,0,1:T(8,128)} fusion(bf16[1408,2048]{0,1:T(8,128)(2,1)} %copy.110, bf16[64,1,32,2048]{3,2,1,0:T(8,128)(2,1)} %all-to-all-done.3, s32[]{:T(128)S(6)} %select_n.15), kind=kOutput, calls=%fused_computation.11 | convolution fusion | flops 2952790016 | bytes 10747908 | tf_op jit(solution)/shard_map/sekd,edf->sekf/dot_general | solution.py:57
  260.6 14.2 %fusion.23 = bf16[16,1,32,2048]{3,2,0,1:T(8,128)(2,1)} fusion(bf16[1,1408,2048]{2,1,0:T(8,128)(2,1)} %all-gather.5.cloned.1.call-done, bf16[1408,2048]{0,1:T(8,128)(2,1)} %copy.111, f32[16,1,32,1408]{3,2,0,1:T(8,128)} %fusion.8, bf16[64,1,32,2048]{3,2,1,0:T(8,128)(2,1)} %all-to-all-done.3, s32[]{:T(128)S(6)} %select_n.15), kind=kOutput, calls=%fused_computation.17 | convolution fusion | flops 5910953984 | bytes 18612228 | tf_op jit(solution)/shard_map/sekf,efd->sekd/dot_general | solution.py:60
  274.8 9.9 %copy.104 = bf16[16,1,32,2048]{2,0,1,3:T(8,128)(2,1)} copy(bf16[16,1,32,2048]{3,2,0,1:T(8,128)(2,1)} %fusion.23) | data formatting | bytes 4194304 | tf_op jit(solution)/shard_map/convert_element_type | solution.py:62
  284.7 10.6 %reshape.141 = bf16[4,2,131072]{2,1,0:T(2,128)(2,1)} reshape(bf16[2048,1,16,32]{3,2,1,0:T(8,128)(2,1)} %bitcast.132) | data formatting | bytes 4194304
  295.3 0.0 all-to-all-done.2
  295.3 4.8 %all-to-all-start.4 = ((bf16[4,2,131072]{2,1,0:T(2,128)(2,1)}), bf16[4,2,131072]{2,1,0:T(2,128)(2,1)}, u32[]{:S(2)}, u32[]{:S(2)}) async-start(bf16[4,2,131072]{2,1,0:T(2,128)(2,1)} %reshape.141), calls=%async_computation.4 | async-start | bytes 4194304 | tf_op jit(solution)/shard_map/all_to_all | solution.py:63
  300.1 3.9 fusion.58
  304.0 6.5 %convolution_convert_fusion.1 = bf16[256,2048]{1,0:T(8,128)(2,1)} fusion(bf16[704,2048]{1,0:T(8,128)(2,1)S(1)} %copy-done, bf16[2048,704]{0,1:T(8,128)(2,1)} %param.20, bf16[256,2048]{0,1:T(8,128)(2,1)} %copy-done.1, f32[256,704]{0,1:T(8,128)} %fusion.58), kind=kOutput, calls=%fused_computation.19 | convolution fusion | flops 1478000640 | bytes 8585216 | tf_op jit(solution)/shard_map/dot_general | solution.py:125
  310.5 2.4 copy.116
  312.9 8.3 %all-to-all-done.4 = bf16[4,2,131072]{2,1,0:T(2,128)(2,1)} async-done(((bf16[4,2,131072]{2,1,0:T(2,128)(2,1)}), bf16[4,2,131072]{2,1,0:T(2,128)(2,1)}, u32[]{:S(2)}, u32[]{:S(2)}) %all-to-all-start.4) | async-done | bytes 2097184 | tf_op jit(solution)/shard_map/all_to_all | solution.py:63
  321.1 5.7 %all-to-all-start.1 = ((bf16[4,256,512]{2,1,0:T(8,128)(2,1)}), bf16[4,256,512]{2,1,0:T(8,128)(2,1)}, u32[]{:S(2)}, u32[]{:S(2)}) async-start(bf16[4,256,512]{2,1,0:T(8,128)(2,1)} %bitcast.136), calls=%async_computation.1 | async-start | bytes 2097152 | tf_op jit(solution)/shard_map/all_to_all | solution.py:46
  326.8 7.4 %reshape.142 = bf16[2048,1,16,32]{3,2,1,0:T(8,128)(2,1)} reshape(bf16[4,2,131072]{2,1,0:T(2,128)(2,1)} %all-to-all-done.4) | data formatting | bytes 4194304
  334.2 9.9 %copy.109 = bf16[16,1,32,4,512]{4,3,2,0,1:T(4,128)(2,1)} copy(bf16[16,1,32,4,512]{2,0,4,3,1:T(8,128)(2,1)} %bitcast.133) | data formatting | bytes 4194304 | tf_op jit(solution)/shard_map/all_to_all | solution.py:63
  344.1 3.4 copy.106
  347.6 0.0 all-to-all-done.1
  347.6 10.4 %all-to-all-start.5 = ((bf16[64,1,32,512]{3,2,1,0:T(8,128)(2,1)}), bf16[64,1,32,512]{3,2,1,0:T(8,128)(2,1)}, u32[]{:S(2)}, u32[]{:S(2)}) async-start(bf16[64,1,32,512]{3,2,1,0:T(8,128)(2,1)} %bitcast.135), calls=%async_computation.5 | async-start | bytes 4194304 | tf_op jit(solution)/shard_map/all_to_all | solution.py:51
  358.0 0.1 copy.108
  358.1 0.1 reshape.127
  358.3 1.5 fusion.57
  359.9 0.1 select_reduce_fusion
  360.0 0.1 copy.95
  360.1 1.5 convert_reduce_fusion
  361.6 47.6 %all-to-all-done.5 = bf16[64,1,32,512]{3,2,1,0:T(8,128)(2,1)} async-done(((bf16[64,1,32,512]{3,2,1,0:T(8,128)(2,1)}), bf16[64,1,32,512]{3,2,1,0:T(8,128)(2,1)}, u32[]{:S(2)}, u32[]{:S(2)}) %all-to-all-start.5) | async-done | bytes 2097184 | tf_op jit(solution)/shard_map/all_to_all | solution.py:51
  409.1 7.0 %gather_fusion = bf16[1024,512]{1,0:T(8,128)(2,1)} fusion(bf16[2048,512]{1,0:T(8,128)(2,1)} %bitcast.36, s32[1024]{0:T(1024)S(1)} %broadcast_clamp_fusion), kind=kCustom, calls=%fused_computation | custom fusion | bytes 2101248 | tf_op jit(solution)/shard_map/gather | solution.py:120
  416.1 2.8 reshape.135
  418.8 3.0 multiply_reduce_fusion
  421.8 0.8 add_convert_fusion
  (25 shorter events, 0.2 us)
Async XLA Ops:
  6.5 297.4 %copy-start = (bf16[704,2048]{1,0:T(8,128)(2,1)S(1)}, bf16[704,2048]{1,0:T(8,128)(2,1)}, u32[]{:S(2)}) copy-start(bf16[704,2048]{1,0:T(8,128)(2,1)} %param.21) | copy-start | bytes 8650756
  6.5 119.1 %all-gather.3.cloned.1.call-start = ((), (), s32[]{:S(2)}) async-start(), calls=%async_computation.6 | async-start | bytes 14417920 | tf_op jit(solution)/shard_map/all_gather | solution.py:31
  10.3 0.9 copy-start.3
  10.4 8.5 %copy-start.5 = (s32[256,4]{0,1:T(4,128)S(1)}, s32[256,4]{0,1:T(4,128)}, u32[]{:S(2)}) copy-start(s32[256,4]{0,1:T(4,128)} %param.15) | copy-start | bytes 12292
  12.5 28.2 %all-to-all-start = ((bf16[4,256,512]{1,2,0:T(8,128)(2,1)}), bf16[4,256,512]{1,2,0:T(8,128)(2,1)}, u32[]{:S(2)}, u32[]{:S(2)}) async-start(bf16[4,256,512]{1,2,0:T(8,128)(2,1)} %broadcast_in_dim.14), calls=%async_computation | async-start | bytes 2097152 | tf_op jit(solution)/shard_map/all_to_all | solution.py:15
  18.8 23.5 %copy-start.6 = (f32[2048]{0:T(1024)S(1)}, f32[2048]{0:T(1024)}, u32[]{:S(2)}) copy-start(f32[2048]{0:T(1024)} %param.12) | copy-start | bytes 24580
  40.7 3.2 copy-start.2
  43.9 5.8 %copy-start.1 = (bf16[256,2048]{0,1:T(8,128)(2,1)}, bf16[256,2048]{0,1:T(8,128)(2,1)S(1)}, u32[]{:S(2)}) copy-start(bf16[256,2048]{0,1:T(8,128)(2,1)S(1)} %fusion.32) | copy-start | bytes 3145732
  49.7 11.7 %copy-start.4 = (bf16[512,60]{0,1:T(8,128)(2,1)S(1)}, bf16[512,60]{0,1:T(8,128)(2,1)}, u32[]{:S(2)}) copy-start(bf16[512,60]{0,1:T(8,128)(2,1)} %param.13) | copy-start | bytes 184324
  49.7 197.1 %all-to-all-start.3 = ((bf16[64,1,32,2048]{3,2,1,0:T(8,128)(2,1)}), bf16[64,1,32,2048]{3,2,1,0:T(8,128)(2,1)}, u32[]{:S(2)}, u32[]{:S(2)}) async-start(bf16[64,1,32,2048]{3,2,1,0:T(8,128)(2,1)} %bitcast.131), calls=%async_computation.3 | async-start | bytes 16777216 | tf_op jit(solution)/shard_map/all_to_all | solution.py:115
  60.6 200.0 %all-gather.5.cloned.1.call-start = ((), (), s32[]{:S(2)}) async-start(), calls=%async_computation.7 | async-start | bytes 7208960 | tf_op jit(solution)/shard_map/all_gather | solution.py:95
  247.5 47.8 %all-to-all-start.2 = ((f32[4,256,60]{1,2,0:T(8,128)}), f32[4,256,60]{1,2,0:T(8,128)S(1)}, u32[]{:S(2)}, u32[]{:S(2)}) async-start(f32[4,256,60]{1,2,0:T(8,128)} %broadcast_in_dim.15), calls=%async_computation.2 | async-start | bytes 524288 | tf_op jit(solution)/shard_map/all_to_all | solution.py:15
  295.3 25.9 %all-to-all-start.4 = ((bf16[4,2,131072]{2,1,0:T(2,128)(2,1)}), bf16[4,2,131072]{2,1,0:T(2,128)(2,1)}, u32[]{:S(2)}, u32[]{:S(2)}) async-start(bf16[4,2,131072]{2,1,0:T(2,128)(2,1)} %reshape.141), calls=%async_computation.4 | async-start | bytes 4194304 | tf_op jit(solution)/shard_map/all_to_all | solution.py:63
  321.1 26.4 %all-to-all-start.1 = ((bf16[4,256,512]{2,1,0:T(8,128)(2,1)}), bf16[4,256,512]{2,1,0:T(8,128)(2,1)}, u32[]{:S(2)}, u32[]{:S(2)}) async-start(bf16[4,256,512]{2,1,0:T(8,128)(2,1)} %bitcast.136), calls=%async_computation.1 | async-start | bytes 2097152 | tf_op jit(solution)/shard_map/all_to_all | solution.py:46
  347.6 10.6 %copy-start.7 = (bf16[2048]{0:T(1024)(128)(2,1)S(1)}, bf16[2048]{0:T(1024)(128)(2,1)}, u32[]{:S(2)}) copy-start(bf16[2048]{0:T(1024)(128)(2,1)} %param.14) | copy-start | bytes 12292
  347.6 61.6 %all-to-all-start.5 = ((bf16[64,1,32,512]{3,2,1,0:T(8,128)(2,1)}), bf16[64,1,32,512]{3,2,1,0:T(8,128)(2,1)}, u32[]{:S(2)}, u32[]{:S(2)}) async-start(bf16[64,1,32,512]{3,2,1,0:T(8,128)(2,1)} %bitcast.135), calls=%async_computation.5 | async-start | bytes 4194304 | tf_op jit(solution)/shard_map/all_to_all | solution.py:51
Sparse Core Ops, SparseCore 0:
  10.5 115.1 all-gather.2
  127.5 64.4 all-gather.4
where the time goes:
time: 431 us; the launch traced here: 429 us
  waiting for transfers between devices  213 us (49%)
  local copies, waits for them, and re-layouts  85.4 us (20%)
  starting transfers between devices  42.9 us (10%)
  matrix products  41.3 us (10%)
  other arithmetic  33.3 us (8%)
  between operations  13.6 us (3%)
    all_to_all x1, waiting for transfers between devices, per_device(): lax.all_to_all(outgoing, 'ep', split_axis=0, concat_axis=0, tiled=True)  93.2 us
    all_gather x1, waiting for transfers between devices, turned_gather(): out, at, done = (lax.all_gather(both, axis, axis=0, tiled=True), 0, [])  63.2 us
    all_to_all x1, waiting for transfers between devices, send_back(): return lax.all_to_all(summed, 'ep', split_axis=0, concat_axis=0, tiled=True)  47.6 us
    unnamed x23, local copies, waits for them, and re-layouts  36.1 us
    another operation x3, other arithmetic  18.2 us
    dot_general x1, matrix products, expert_rows(): jnp.einsum('sekf,efd->sekd', hidden, w_down, preferred_element_type=jnp.f...  14.2 us
    all_to_all x2, local copies, waits for them, and re-layouts, expert_rows(): lax.all_to_all(full_out, 'tp', split_axis=3, concat_axis=0, tiled=True)  13.4 us
    all_to_all x2, starting transfers between devices, copy_for_each(): lax.all_to_all(jnp.broadcast_to(value[None], (peers, *value.shape)), axis...  11.2 us
  transfers between devices with their start and end apart: 8, of which 4 were waited for; matrix products, arithmetic and copies ran while one was open for 33% of the time, Pallas kernels for 0%

commit v1 on v0

--- a/solution.py
+++ b/solution.py
@@ -1,7 +1,34 @@
+import functools
 import jax
 import jax.numpy as jnp
 from jax import lax
 from jax.sharding import PartitionSpec as P
+from jax.lax import axis_index, axis_size, ppermute
+
+
+def press_panels(chunk, shard_axis):
+    prior = axis_size(shard_axis)
+    reached = axis_index(shard_axis)
+    local_out, response = (prior, reached)
+    w_next = chunk.shape[3] // local_out
+    x_new = list(chunk.shape)
+    x_new[3] = w_next
+    high = x_new[0]
+    x_new[0] = high * local_out
+    res = jnp.zeros(x_new, chunk.dtype)
+    q = 0
+    while q < local_out:
+        carry_in = lax.dynamic_slice_in_dim(chunk, (response ^ q) * w_next, w_next, axis=3)
+        if q:
+            carry_in = ppermute(
+                carry_in, axis_name=shard_axis, perm=[(to_i, to_i ^ q) for to_i in range(local_out)]
+            )
+        res = lax.dynamic_update_slice_in_dim(res, carry_in, (response ^ q) * high, axis=0)
+        q = q + 1
+    return res
+
+
+map_works = functools.partial(press_panels, shard_axis="tp")
 
 
 def laid_out(parts, dim):
@@ -60,7 +87,7 @@
     full_out = jnp.einsum(
         "sekf,efd->sekd", hidden, w_down, preferred_element_type=jnp.float32
     ).astype(jnp.bfloat16)
-    summed = lax.all_to_all(full_out, "tp", split_axis=3, concat_axis=0, tiled=True)
+    summed = map_works(full_out)
     return send_back(summed)
 
 

time: 431 us -> 406 us (0.942)
  local copies, waits for them, and re-layouts: 85.4 us -> 55.8 us
    unnamed x23 -> x21, local copies, waits for them, and re-layouts: 36.1 us -> 18.1 us
    all_to_all x2 -> x0, local copies, waits for them, and re-layouts: 13.4 us -> none  [expert_rows(): lax.all_to_all(full_out, 'tp', split_axis=3, concat_axis=0, tiled=True)]
    ppermute x0 -> x3, waiting for transfers between devices: none -> 13 us  [press_panels(): ppermute(carry_in, axis_name=shard_axis, perm=[(to_i, to_i ^ q) for to_i...]
    convert_element_type x1 -> x0, local copies, waits for them, and re-layouts: 9.95 us -> none  [expert_rows(): full_out = jnp.einsum('sekf,efd->sekd', hidden, w_down, preferred_element...]
    all_to_all x1 -> x0, waiting for transfers between devices: 8.27 us -> none  [expert_rows(): lax.all_to_all(full_out, 'tp', split_axis=3, concat_axis=0, tiled=True)]
    dynamic_update_slice x0 -> x4, local copies, waits for them, and re-layouts: none -> 7.56 us  [press_panels(): lax.dynamic_update_slice_in_dim(res, carry_in, (response ^ q) * high, axi...]
    all_to_all x1 -> x0, starting transfers between devices: 4.8 us -> none  [expert_rows(): lax.all_to_all(full_out, 'tp', split_axis=3, concat_axis=0, tiled=True)]
  transfers between devices with their start and end apart: 8 -> 10, of which waited for: 4 -> 6; matrix products, arithmetic and copies ran while one was open for 33% -> 28% of each run, Pallas kernels for 0% -> 0%
where the time goes in v1:
time: 406 us; the launch traced here: 402 us
  waiting for transfers between devices  215 us (53%)
  local copies, waits for them, and re-layouts  55.8 us (14%)
  starting transfers between devices  43.7 us (11%)
  matrix products  41.3 us (10%)
  other arithmetic  33.3 us (8%)
  between operations  13.7 us (3%)
    all_to_all x1, waiting for transfers between devices, per_device(): lax.all_to_all(outgoing, 'ep', split_axis=0, concat_axis=0, tiled=True)  93.2 us
    all_gather x1, waiting for transfers between devices, turned_gather(): out, at, done = (lax.all_gather(both, axis, axis=0, tiled=True), 0, [])  59.2 us
    all_to_all x1, waiting for transfers between devices, send_back(): return lax.all_to_all(summed, 'ep', split_axis=0, concat_axis=0, tiled=True)  47.6 us
    another operation x3, other arithmetic  18.2 us
    unnamed x21, local copies, waits for them, and re-layouts  18.1 us
    dot_general x1, matrix products, expert_rows(): jnp.einsum('sekf,efd->sekd', hidden, w_down, preferred_element_type=jnp.f...  14.1 us
    ppermute x3, waiting for transfers between devices, press_panels(): ppermute(carry_in, axis_name=shard_axis, perm=[(to_i, to_i ^ q) for to_i...  13 us
    all_to_all x1, starting transfers between devices, send_back(): return lax.all_to_all(summed, 'ep', split_axis=0, concat_axis=0, tiled=True)  12.4 us
  transfers between devices with their start and end apart: 10, of which 6 were waited for; matrix products, arithmetic and copies ran while one was open for 28% of the time, Pallas kernels for 0%

profile of v1, /device:TPU:8, one launch (start us, length us, event | category | flops | bytes accessed | tf_op | source)
XLA Modules:
  0.0 402.4 jit_solution(17261211205655108749)
XLA Ops:
  6.5 3.8 pad_maximum_fusion
  10.4 0.0 all-gather.3.cloned.1.call-update
  10.4 0.9 copy-done.3
  11.3 0.1 copy.78
  11.4 1.0 broadcast_in_dim.16
  12.5 6.4 %all-to-all-start = ((bf16[4,256,512]{1,2,0:T(8,128)(2,1)}), bf16[4,256,512]{1,2,0:T(8,128)(2,1)}, u32[]{:S(2)}, u32[]{:S(2)}) async-start(bf16[4,256,512]{1,2,0:T(8,128)(2,1)} %broadcast_in_dim.16), calls=%async_computation | async-start | bytes 2097152 | tf_op jit(solution)/shard_map/all_to_all | solution.py:42
  18.8 0.1 copy.82
  19.0 0.1 eq.58
  19.1 0.1 eq.54
  19.2 18.0 %reduce-window.6 = s32[64,8,128]{2,1,0:T(8,128)S(1)} reduce-window(s32[64,8,128]{2,1,0:T(8,128)S(1)} %fusion.44, s32[]{:T(128)} %constant.20.clone.1), window={size=1x1x128 pad=0_0x0_0x127_0}, to_apply=%region_6.7 | reduce-window | flops 8323072 | bytes 524292 | tf_op jit(solution)/shard_map/reduce-window
  37.3 0.1 slice.19
  37.4 0.1 copy.84
  37.6 0.1 copy.85
  37.7 0.1 broadcast_add_fusion
  37.8 0.1 fusion.41
  37.9 0.1 reduce_sum.83
  38.0 0.1 copy.86
  38.1 2.5 fusion.7
  40.6 0.0 all-to-all-done
  40.7 1.6 multiply_reduce_fusion.1
  42.3 1.6 fusion.29
  43.9 5.8 %convolution_convert_fusion = bf16[2048,2048]{1,0:T(8,128)(2,1)} fusion(bf16[2048,256]{1,0:T(8,128)(2,1)S(1)} %copy-done.2, bf16[256,2048]{0,1:T(8,128)(2,1)S(1)} %fusion.29), kind=kOutput, calls=%fused_computation.3 | convolution fusion | flops 2151677952 | bytes 10485760 | tf_op jit(solution)/shard_map/dot_general | solution.py:137
  49.7 10.9 %all-to-all-start.3 = ((bf16[64,1,32,2048]{3,2,1,0:T(8,128)(2,1)}), bf16[64,1,32,2048]{3,2,1,0:T(8,128)(2,1)}, u32[]{:S(2)}, u32[]{:S(2)}) async-start(bf16[64,1,32,2048]{3,2,1,0:T(8,128)(2,1)} %bitcast.148), calls=%async_computation.3 | async-start | bytes 16777216 | tf_op jit(solution)/shard_map/all_to_all | solution.py:142
  60.6 0.0 all-gather.5.cloned.1.call-start
  60.6 0.7 all-gather.5.cloned.1.call-update
  61.4 1.1 fusion.42
  62.5 3.9 fusion.55
  66.4 59.2 %all-gather.3.cloned.1.call-done = bf16[1408,4096]{1,0:T(8,128)(2,1)} async-done(((bf16[352,4096]{1,0:T(8,128)(2,1)}), bf16[1408,4096]{1,0:T(8,128)(2,1)}) %all-gather.3.cloned.1.call-update) | async-done | bytes 11534352 | tf_op jit(solution)/shard_map/all_gather | solution.py:58
  125.7 11.0 %fusion.53 = (bf16[1408,2048]{1,0:T(8,128)(2,1)}, bf16[1408,2048]{1,0:T(8,128)(2,1)}) fusion(bf16[1408,4096]{1,0:T(8,128)(2,1)} %all-gather.3.cloned.1.call-done), kind=kLoop, calls=%fused_computation.67 | loop fusion | bytes 23068672 | tf_op jit(solution)/shard_map/slice | solution.py:60
  136.6 8.5 %copy.94 = bf16[1408,2048]{0,1:T(8,128)(2,1)} copy(bf16[1408,2048]{1,0:T(8,128)(2,1)} %get-tuple-element.7) | data formatting | bytes 11534336
  145.2 8.4 %copy.95 = bf16[1408,2048]{0,1:T(8,128)(2,1)} copy(bf16[1408,2048]{1,0:T(8,128)(2,1)} %get-tuple-element.8) | data formatting | bytes 11534336
  153.5 93.2 %all-to-all-done.3 = bf16[64,1,32,2048]{3,2,1,0:T(8,128)(2,1)} async-done(((bf16[64,1,32,2048]{3,2,1,0:T(8,128)(2,1)}), bf16[64,1,32,2048]{3,2,1,0:T(8,128)(2,1)}, u32[]{:S(2)}, u32[]{:S(2)}) %all-to-all-start.3) | async-done | bytes 8388640 | tf_op jit(solution)/shard_map/all_to_all | solution.py:142
  246.8 0.7 broadcast_in_dim.17
  247.5 4.8 %all-to-all-start.2 = ((f32[4,256,60]{1,2,0:T(8,128)}), f32[4,256,60]{1,2,0:T(8,128)S(1)}, u32[]{:S(2)}, u32[]{:S(2)}) async-start(f32[4,256,60]{1,2,0:T(8,128)} %broadcast_in_dim.17), calls=%async_computation.2 | async-start | bytes 524288 | tf_op jit(solution)/shard_map/all_to_all | solution.py:42
  252.3 8.3 %fusion.8 = f32[16,1,32,1408]{3,2,0,1:T(8,128)} fusion(bf16[1408,2048]{0,1:T(8,128)(2,1)} %copy.94, bf16[64,1,32,2048]{3,2,1,0:T(8,128)(2,1)} %all-to-all-done.3, s32[]{:T(128)S(6)} %select_n.35), kind=kOutput, calls=%fused_computation.11 | convolution fusion | flops 2952790016 | bytes 10747908 | tf_op jit(solution)/shard_map/sekd,edf->sekf/dot_general | solution.py:84
  260.6 14.1 %fusion.17 = bf16[16,32,2048]{2,1,0:T(8,128)(2,1)} fusion(bf16[1,1408,2048]{2,1,0:T(8,128)(2,1)} %all-gather.5.cloned.1.call-done, bf16[1408,2048]{0,1:T(8,128)(2,1)} %copy.95, f32[16,1,32,1408]{3,2,0,1:T(8,128)} %fusion.8, bf16[64,1,32,2048]{3,2,1,0:T(8,128)(2,1)} %all-to-all-done.3, s32[]{:T(128)S(6)} %select_n.35), kind=kOutput, calls=%fused_computation.14 | convolution fusion | flops 5910953984 | bytes 18612228 | tf_op jit(solution)/shard_map/sekf,efd->sekd/dot_general | solution.py:87
  274.7 2.6 dynamic-slice_bitcast_fusion
  277.3 0.0 collective-permute-start
  277.3 2.9 collective-permute-start.1
  280.2 6.6 %convolution_convert_fusion.1 = bf16[256,2048]{1,0:T(8,128)(2,1)} fusion(bf16[704,2048]{1,0:T(8,128)(2,1)S(1)} %copy-done, bf16[2048,704]{0,1:T(8,128)(2,1)} %param.20, bf16[256,2048]{0,1:T(8,128)(2,1)} %copy-done.1, f32[256,704]{0,1:T(8,128)} %fusion.55), kind=kOutput, calls=%fused_computation.18 | convolution fusion | flops 1478000640 | bytes 8585216 | tf_op jit(solution)/shard_map/dot_general | solution.py:152
  286.8 2.3 copy.100
  289.1 0.6 collective-permute-start.2
  289.7 5.7 %all-to-all-start.1 = ((bf16[4,256,512]{2,1,0:T(8,128)(2,1)}), bf16[4,256,512]{2,1,0:T(8,128)(2,1)}, u32[]{:S(2)}, u32[]{:S(2)}) async-start(bf16[4,256,512]{2,1,0:T(8,128)(2,1)} %bitcast.149), calls=%async_computation.1 | async-start | bytes 2097152 | tf_op jit(solution)/shard_map/all_to_all | solution.py:73
  295.4 1.5 broadcast_in_dim.24
  296.9 1.9 bitcast_dynamic-update-slice_fusion
  298.8 0.0 collective-permute-done
  298.8 1.9 bitcast_dynamic-update-slice_fusion.3
  300.7 3.8 collective-permute-done.1
  304.5 1.9 bitcast_dynamic-update-slice_fusion.2
  306.4 9.2 %collective-permute-done.2 = bf16[16,1,32,512]{3,2,0,1:T(8,128)(2,1)} collective-permute-done((bf16[16,1,32,512]{3,2,0,1:T(8,128)(2,1)}, bf16[16,1,32,512]{3,2,0,1:T(8,128)(2,1)}, u32[]{:S(2)}, u32[]{:S(2)}) %collective-permute-start.2) | collective-permute-done | bytes 524320 | tf_op jit(solution)/shard_map/ppermute | solution.py:23
  315.6 1.9 bitcast_dynamic-update-slice_fusion.1
  317.5 0.9 all-to-all-done.1
  318.4 12.4 %all-to-all-start.4 = ((bf16[64,1,32,512]{3,2,1,0:T(8,128)(2,1)}), bf16[64,1,32,512]{3,2,1,0:T(8,128)(2,1)}, u32[]{:S(2)}, u32[]{:S(2)}) async-start(bf16[64,1,32,512]{3,2,1,0:T(8,128)(2,1)} %bitcast_dynamic-update-slice_fusion.1), calls=%async_computation.4 | async-start | bytes 4194304 | tf_op jit(solution)/shard_map/all_to_all | solution.py:78
  330.8 0.1 copy.93
  331.0 0.1 reshape.143
  331.2 1.5 fusion.54
  332.8 0.1 select_reduce_fusion
  332.9 0.1 copy.80
  333.0 1.5 convert_reduce_fusion
  334.5 47.6 %all-to-all-done.4 = bf16[64,1,32,512]{3,2,1,0:T(8,128)(2,1)} async-done(((bf16[64,1,32,512]{3,2,1,0:T(8,128)(2,1)}), bf16[64,1,32,512]{3,2,1,0:T(8,128)(2,1)}, u32[]{:S(2)}, u32[]{:S(2)}) %all-to-all-start.4) | async-done | bytes 2097184 | tf_op jit(solution)/shard_map/all_to_all | solution.py:78
  382.0 7.0 %gather_fusion = bf16[1024,512]{1,0:T(8,128)(2,1)} fusion(bf16[2048,512]{1,0:T(8,128)(2,1)} %bitcast.45, s32[1024]{0:T(1024)S(1)} %broadcast_clamp_fusion), kind=kCustom, calls=%fused_computation | custom fusion | bytes 2101248 | tf_op jit(solution)/shard_map/gather | solution.py:147
  389.0 2.8 reshape.151
  391.7 3.0 multiply_reduce_fusion
  394.7 0.8 add_convert_fusion
  (30 shorter events, 0.2 us)
Async XLA Ops:
  6.5 273.7 %copy-start = (bf16[704,2048]{1,0:T(8,128)(2,1)S(1)}, bf16[704,2048]{1,0:T(8,128)(2,1)}, u32[]{:S(2)}) copy-start(bf16[704,2048]{1,0:T(8,128)(2,1)} %param.21) | copy-start | bytes 8650756
  6.5 119.1 %all-gather.3.cloned.1.call-start = ((), (), s32[]{:S(2)}) async-start(), calls=%async_computation.5 | async-start | bytes 14417920 | tf_op jit(solution)/shard_map/all_gather | solution.py:58
  10.3 0.9 copy-start.3
  10.4 8.5 %copy-start.5 = (s32[256,4]{0,1:T(4,128)S(1)}, s32[256,4]{0,1:T(4,128)}, u32[]{:S(2)}) copy-start(s32[256,4]{0,1:T(4,128)} %param.15) | copy-start | bytes 12292
  12.5 28.2 %all-to-all-start = ((bf16[4,256,512]{1,2,0:T(8,128)(2,1)}), bf16[4,256,512]{1,2,0:T(8,128)(2,1)}, u32[]{:S(2)}, u32[]{:S(2)}) async-start(bf16[4,256,512]{1,2,0:T(8,128)(2,1)} %broadcast_in_dim.16), calls=%async_computation | async-start | bytes 2097152 | tf_op jit(solution)/shard_map/all_to_all | solution.py:42
  18.8 23.5 %copy-start.6 = (f32[2048]{0:T(1024)S(1)}, f32[2048]{0:T(1024)}, u32[]{:S(2)}) copy-start(f32[2048]{0:T(1024)} %param.12) | copy-start | bytes 24580
  40.7 3.2 copy-start.2
  43.9 5.8 %copy-start.1 = (bf16[256,2048]{0,1:T(8,128)(2,1)}, bf16[256,2048]{0,1:T(8,128)(2,1)S(1)}, u32[]{:S(2)}) copy-start(bf16[256,2048]{0,1:T(8,128)(2,1)S(1)} %fusion.29) | copy-start | bytes 3145732
  49.7 11.7 %copy-start.4 = (bf16[512,60]{0,1:T(8,128)(2,1)S(1)}, bf16[512,60]{0,1:T(8,128)(2,1)}, u32[]{:S(2)}) copy-start(bf16[512,60]{0,1:T(8,128)(2,1)} %param.13) | copy-start | bytes 184324
  49.7 197.1 %all-to-all-start.3 = ((bf16[64,1,32,2048]{3,2,1,0:T(8,128)(2,1)}), bf16[64,1,32,2048]{3,2,1,0:T(8,128)(2,1)}, u32[]{:S(2)}, u32[]{:S(2)}) async-start(bf16[64,1,32,2048]{3,2,1,0:T(8,128)(2,1)} %bitcast.148), calls=%async_computation.3 | async-start | bytes 16777216 | tf_op jit(solution)/shard_map/all_to_all | solution.py:142
  60.6 200.0 %all-gather.5.cloned.1.call-start = ((), (), s32[]{:S(2)}) async-start(), calls=%async_computation.6 | async-start | bytes 7208960 | tf_op jit(solution)/shard_map/all_gather | solution.py:122
  247.5 42.2 %all-to-all-start.2 = ((f32[4,256,60]{1,2,0:T(8,128)}), f32[4,256,60]{1,2,0:T(8,128)S(1)}, u32[]{:S(2)}, u32[]{:S(2)}) async-start(f32[4,256,60]{1,2,0:T(8,128)} %broadcast_in_dim.17), calls=%async_computation.2 | async-start | bytes 524288 | tf_op jit(solution)/shard_map/all_to_all | solution.py:42
  277.3 21.6 %collective-permute-start = (bf16[16,1,32,512]{3,2,0,1:T(8,128)(2,1)}, bf16[16,1,32,512]{3,2,0,1:T(8,128)(2,1)}, u32[]{:S(2)}, u32[]{:S(2)}) collective-permute-start(bf16[16,1,32,512]{3,2,0,1:T(8,128)(2,1)} %get-tuple-element.11), channel_id=1, source_target_pairs={{0,1},{1,0},{2,3},{3,2},{4,5},{5,4},{6,7},{7,6},{8,9},{9,8},{10,11... | collective-permute-start | bytes 1572872 | tf_op jit(solution)/shard_map/ppermute | solution.py:23
  277.3 27.3 %collective-permute-start.1 = (bf16[16,1,32,512]{3,2,0,1:T(8,128)(2,1)}, bf16[16,1,32,512]{3,2,0,1:T(8,128)(2,1)}, u32[]{:S(2)}, u32[]{:S(2)}) collective-permute-start(bf16[16,1,32,512]{3,2,0,1:T(8,128)(2,1)} %get-tuple-element.10), channel_id=1, source_target_pairs={{0,2},{1,3},{2,0},{3,1},{4,6},{5,7},{6,4},{7,5},{8,10},{9,11},{10,... | collective-permute-start | bytes 1572872 | tf_op jit(solution)/shard_map/ppermute | solution.py:23
  289.1 26.5 %collective-permute-start.2 = (bf16[16,1,32,512]{3,2,0,1:T(8,128)(2,1)}, bf16[16,1,32,512]{3,2,0,1:T(8,128)(2,1)}, u32[]{:S(2)}, u32[]{:S(2)}) collective-permute-start(bf16[16,1,32,512]{3,2,0,1:T(8,128)(2,1)} %get-tuple-element.9), channel_id=1, source_target_pairs={{0,3},{1,2},{2,1},{3,0},{4,7},{5,6},{6,5},{7,4},{8,11},{9,10},{10,... | collective-permute-start | bytes 1572872 | tf_op jit(solution)/shard_map/ppermute | solution.py:23
  289.7 28.7 %all-to-all-start.1 = ((bf16[4,256,512]{2,1,0:T(8,128)(2,1)}), bf16[4,256,512]{2,1,0:T(8,128)(2,1)}, u32[]{:S(2)}, u32[]{:S(2)}) async-start(bf16[4,256,512]{2,1,0:T(8,128)(2,1)} %bitcast.149), calls=%async_computation.1 | async-start | bytes 2097152 | tf_op jit(solution)/shard_map/all_to_all | solution.py:73
  306.4 24.7 %copy-start.7 = (bf16[2048]{0:T(1024)(128)(2,1)S(1)}, bf16[2048]{0:T(1024)(128)(2,1)}, u32[]{:S(2)}) copy-start(bf16[2048]{0:T(1024)(128)(2,1)} %param.14) | copy-start | bytes 12292
  318.4 63.6 %all-to-all-start.4 = ((bf16[64,1,32,512]{3,2,1,0:T(8,128)(2,1)}), bf16[64,1,32,512]{3,2,1,0:T(8,128)(2,1)}, u32[]{:S(2)}, u32[]{:S(2)}) async-start(bf16[64,1,32,512]{3,2,1,0:T(8,128)(2,1)} %bitcast_dynamic-update-slice_fusion.1), calls=%async_computation.4 | async-start | bytes 4194304 | tf_op jit(solution)/shard_map/all_to_all | solution.py:78
Sparse Core Ops, SparseCore 0:
  10.5 115.1 all-gather.2
  127.5 64.4 all-gather.4
